TPU v7x, 768 devices: a whole 4x8x12 slice. The times are simulated.
768 devices in a mesh: dp: 24 (over z_hi, y), seq: 16 (over z_lo, x), mp: 2 (over core).
Axes of the slice: x: 4, y: 8, z: 12 (z_hi: 3, z_lo: 4; z = z_hi * 4 + z_lo), core: 2. Of those that a mesh axis runs over, the one named last changes fastest.
Arguments:
- features: bfloat16 [24, 32, 32, 16, 256], P('dp', 'seq'), may hold values from -6 to 6
- conv_weight: bfloat16 [3, 3, 3, 256, 256], replicated, may hold values from -0.078125 to 0.078125
- latent_weight: bfloat16 [256, 16], replicated, may hold values from -0.375 to 0.375
- order: int32 [256], replicated, may hold values from 0 to 255, each once
- embed_weight: bfloat16 [64, 6144], P(None, 'mp'), may hold values from -0.75 to 0.75
- cotangent: bfloat16 [98304, 6144], P(('dp', 'seq'), 'mp'), may hold values from -0.078125 to 0.078125
Outputs:
- embedded: bfloat16 [98304, 6144], P(('dp', 'seq'), 'mp')
- embed_grad: float32 [2, 64, 3072], P('mp', None, ('dp', 'seq'))
Inputs may be any that keep to these rules, and one draw needn't show every extreme that they name: order is a permutation of the positions of a band.
All inputs are finite; a program needn't handle non-finite values.
Results may differ from a plain program's by a relative error of at most 0.0058.
Values may be sent and summed in bfloat16 or wider, within the bound.
A program may use at most 32 MiB of HBM per device.

v0:
```python
import jax
import jax.numpy as jnp
from jax import lax
from jax.sharding import PartitionSpec as P


def passed_along(value, axis, steps):
    count = lax.axis_size(axis)
    initial, last = (max(0, -steps), min(count, count - steps))
    return lax.ppermute(value, axis, [(source, source + steps) for source in range(initial, last)])


def split_up(value, dim, peers):
    lengths = value.shape
    pieces = value.reshape(*lengths[:dim], peers, lengths[dim] // peers, *lengths[dim + 1 :])
    return jnp.moveaxis(pieces, dim, 0)


def summed_on_arrival(value, axis, dim):
    peers = lax.axis_size(axis)
    pieces = lax.all_to_all(split_up(value, dim, peers), axis, 0, 0, tiled=True)
    return jnp.sum(pieces, axis=0)


def local(features, conv_weight, latent_weight, order, embed_weight, cotangent):
    before = passed_along(features, "seq", 1)
    widened = jnp.concatenate([before, features], axis=1)
    conv = lax.conv_general_dilated(
        widened,
        conv_weight,
        (1, 1, 1),
        ((0, 0), (1, 1), (1, 1)),
        dimension_numbers=("NDHWC", "DHWIO", "NDHWC"),
        preferred_element_type=jnp.float32,
    )
    activated = (features.astype(jnp.float32) + jax.nn.silu(conv)).astype(jnp.bfloat16)
    frames = features.shape[1]
    rows = features.shape[2] // 2
    cols = features.shape[3] // 2
    channels = features.shape[4]
    latent = jnp.dot(
        activated.reshape(-1, channels), latent_weight, preferred_element_type=jnp.float32
    ).astype(jnp.bfloat16)
    latent_ch = latent_weight.shape[1]
    patches = latent.reshape(frames, rows, 2, cols, 2, latent_ch).transpose(0, 1, 3, 2, 4, 5)
    patches = patches.reshape(frames, rows, cols, 4 * latent_ch)
    banded = lax.all_to_all(patches, "seq", split_axis=1, concat_axis=0, tiled=True)
    local_tok = banded.reshape(-1, 4 * latent_ch)
    tokens = jnp.take(local_tok, order, axis=0)
    embedded = jnp.dot(tokens, embed_weight, preferred_element_type=jnp.float32).astype(
        jnp.bfloat16
    )
    partial_grad = jnp.dot(tokens.T, cotangent, preferred_element_type=jnp.float32)
    halfway = summed_on_arrival(partial_grad, "dp", 1)
    summed = summed_on_arrival(halfway, "seq", 1)
    return (embedded, summed[None])


def solution(mesh):
    placed = (
        P("dp", "seq", None, None, None),
        P(),
        P(),
        P(),
        P(None, "mp"),
        P(("dp", "seq"), "mp"),
    )
    return jax.shard_map(
        local,
        mesh=mesh,
        in_specs=placed,
        out_specs=(P(("dp", "seq"), "mp"), P("mp", None, ("dp", "seq"))),
        check_vma=False,
    )
```

profile of v0, /device:TPU:8, one launch (start us, length us, event | category | flops | bytes accessed | tf_op | source)
XLA Modules:
  0.0 133.6 jit_solution(2941461133424923101)
XLA Ops:
  0.6 0.0 copy-start
  0.6 1.4 %copy.27 = bf16[1,2,32,16,256]{4,2,3,1,0:T(8,128)(2,1)S(1)} copy(bf16[1,2,32,16,256]{4,3,2,1,0:T(8,128)(2,1)} %param.6) | data formatting | bytes 1048576 | tf_op args[0]
  2.0 3.4 %collective-permute-start = (bf16[1,2,32,16,256]{4,2,3,1,0:T(8,128)(2,1)S(1)}, bf16[1,2,32,16,256]{4,2,3,1,0:T(8,128)(2,1)S(1)}, u32[]{:S(2)}, u32[]{:S(2)}) collective-permute-start(bf16[1,2,32,16,256]{4,2,3,1,0:T(8,128)(2,1)S(1)} %copy.27), channel_id=1, source_target_pairs={{0,2},{2,4},{4,6},{6,8},{8,10},{10,12},{12,14},{14,16},{16,18},{18... | collective-permute-start | bytes 1572872 | tf_op jit(solution)/shard_map/ppermute | solution.py:10
  5.4 0.7 compare_and_fusion
  6.1 0.7 compare_select_fusion
  6.8 9.8 %collective-permute-done = bf16[1,2,32,16,256]{4,2,3,1,0:T(8,128)(2,1)S(1)} collective-permute-done((bf16[1,2,32,16,256]{4,2,3,1,0:T(8,128)(2,1)S(1)}, bf16[1,2,32,16,256]{4,2,3,1,0:T(8,128)(2,1)S(1)}, u32[]{:S(2)}, u32[]{:S(2)}) %collective-permute-start) | collective-permute-done | bytes 524320 | tf_op jit(solution)/shard_map/ppermute | solution.py:10
  16.6 0.1 maximum_bitcast_fusion
  16.7 0.2 pad
  16.9 0.9 copy.31
  17.8 0.0 copy-start.3
  17.8 0.2 slice.4
  18.0 0.0 copy-done
  18.0 0.4 copy-done.3
  18.4 6.2 %divide_multiply_fusion = f32[2,32,8,3,256]{4,2,3,1,0:T(8,128)S(1)} fusion(bf16[3,3,3,256,256]{4,3,2,1,0:T(8,128)(2,1)S(1)} %copy-done, bf16[4,32,1,7,2,256]{5,3,4,1,0,2:T(8,128)(2,1)S(1)} %slice.4, bf16[4,32,1,8,3,256]{5,3,4,1,0,2:T(8,128)(2,1)S(1)} %copy.31, pred[8,3]{0,1:T(4,128)(4,1)S(1)} %copy-done.3), kind=kOutput, calls=%fused_computation.10 | convolution fusion | flops 5332402176 | bytes 7602200 | tf_op jit(solution)/shard_map/conv_general_dilated | solution.py:28
  24.7 0.0 copy-start.1
  24.7 0.5 copy.32
  25.2 0.6 copy-done.1
  25.7 0.0 copy-start.2
  25.7 0.2 fusion.12
  26.0 0.3 copy.33
  26.3 0.1 copy-done.2
  26.4 0.9 convolution_convert_fusion.1
  27.3 1.6 %copy.34 = bf16[1024,16]{1,0:T(8,128)(2,1)} copy(bf16[1024,16]{0,1:T(8,128)(2,1)} %convolution_convert_fusion.1) | data formatting | bytes 65536 | tf_op jit(solution)/shard_map/convert_element_type | solution.py:43
  28.9 1.9 %copy.40 = bf16[2,16,8,2,2,16]{5,4,3,2,0,1:T(2,128)(2,1)} copy(bf16[2,16,8,2,2,16]{5,4,2,3,1,0:T(2,128)(2,1)} %bitcast.55) | data formatting | bytes 65536 | tf_op jit(solution)/shard_map/reshape | solution.py:46
  30.8 1.8 %reshape.55 = bf16[2,16,8,64]{3,2,0,1:T(8,128)(2,1)} reshape(bf16[2,16,8,2,2,16]{5,4,3,2,0,1:T(2,128)(2,1)} %copy.40) | data formatting | bytes 65536 | tf_op jit(solution)/shard_map/reshape | solution.py:46
  32.6 1.6 %reshape.56 = bf16[16,2,512]{2,1,0:T(2,128)(2,1)} reshape(bf16[16,2,8,64]{3,2,1,0:T(8,128)(2,1)} %bitcast.56) | data formatting | bytes 65536
  34.1 10.9 %all-to-all-start = ((bf16[16,2,512]{2,1,0:T(2,128)(2,1)}), bf16[16,2,512]{2,1,0:T(2,128)(2,1)}, u32[]{:S(2)}, u32[]{:S(2)}) async-start(bf16[16,2,512]{2,1,0:T(2,128)(2,1)} %reshape.56), calls=%async_computation | async-start | bytes 65536 | tf_op jit(solution)/shard_map/all_to_all | solution.py:47
  45.0 8.2 %all-to-all-done = bf16[16,2,512]{2,1,0:T(2,128)(2,1)} async-done(((bf16[16,2,512]{2,1,0:T(2,128)(2,1)}), bf16[16,2,512]{2,1,0:T(2,128)(2,1)}, u32[]{:S(2)}, u32[]{:S(2)}) %all-to-all-start) | async-done | bytes 32800 | tf_op jit(solution)/shard_map/all_to_all | solution.py:47
  53.2 1.5 %reshape.57 = bf16[16,2,8,64]{3,2,1,0:T(8,128)(2,1)} reshape(bf16[16,2,512]{2,1,0:T(2,128)(2,1)} %all-to-all-done) | data formatting | bytes 65536
  54.7 2.2 %gather_fusion = bf16[256,64]{1,0:T(8,128)(2,1)} fusion(bf16[256,64]{1,0:T(8,128)(2,1)} %bitcast.51, s32[1024]{0:T(1024)S(1)} %pad_clamp_fusion), kind=kCustom, calls=%fused_computation | custom fusion | bytes 66560 | tf_op jit(solution)/shard_map/jit(_take)/gather | solution.py:49
  56.9 1.9 %convolution_bitcast_fusion = f32[8,24,8,128]{3,2,1,0:T(8,128)S(1)} fusion(bf16[256,3072]{1,0:T(8,128)(2,1)} %param.11, bf16[256,64]{1,0:T(8,128)(2,1)} %gather_fusion, pred[256]{0:T(512)(128)(4,1)S(1)} %compare_and_fusion), kind=kOutput, calls=%fused_computation.12 | convolution fusion | flops 100679680 | bytes 2392320 | tf_op jit(solution)/shard_map/dot_general | solution.py:53
  58.8 0.1 copy.46
  58.9 50.7 %all_to_all.25 = f32[24,64,128]{2,1,0:T(8,128)} all-to-all(f32[24,64,128]{2,1,0:T(8,128)S(1)} %bitcast.53), channel_id=1, replica_groups=mesh['dp'=24,'seq'=16,'mp'=2] {'dp'}, dimensions={0} | all-to-all | bytes 1572864 | tf_op jit(solution)/shard_map/all_to_all | solution.py:21
  109.6 1.8 %reduce_sum.18 = f32[64,128]{1,0:T(8,128)} reduce(f32[24,64,128]{2,1,0:T(8,128)} %all_to_all.25, f32[]{:T(128)} %constant.20.clone.1), dimensions={0}, to_apply=%region_0.1 | reduce | flops 188416 | bytes 819204 | tf_op jit(solution)/shard_map/reduce_sum | solution.py:22
  111.4 1.5 %copy.39 = f32[64,128]{0,1:T(8,128)} copy(f32[64,128]{1,0:T(8,128)} %reduce_sum.18) | data formatting | bytes 65536 | tf_op jit(solution)/shard_map/reduce_sum | solution.py:22
  112.9 1.5 %bitcast_bitcast_fusion.1 = f32[16,8,64]{2,1,0:T(8,128)} fusion(f32[64,128]{0,1:T(8,128)} %copy.39), kind=kLoop, calls=%fused_computation.29 | loop fusion | bytes 65536
  114.3 1.5 %reshape.58 = f32[16,1,512]{2,1,0:T(1,128)} reshape(f32[16,8,64]{2,1,0:T(8,128)} %bitcast_bitcast_fusion.1) | data formatting | bytes 65536
  115.9 4.1 %all-to-all-start.2 = ((f32[16,1,512]{2,1,0:T(1,128)}), f32[16,1,512]{2,1,0:T(1,128)}, u32[]{:S(2)}, u32[]{:S(2)}) async-start(f32[16,1,512]{2,1,0:T(1,128)} %reshape.58), calls=%async_computation.2 | async-start | bytes 65536 | tf_op jit(solution)/shard_map/all_to_all | solution.py:21
  120.0 2.8 %convolution_convert_fusion = bf16[256,3072]{1,0:T(8,128)(2,1)} fusion(bf16[64,3072]{1,0:T(8,128)(2,1)} %param.10, bf16[256,64]{1,0:T(8,128)(2,1)} %gather_fusion, pred[256]{0:T(512)(128)(4,1)S(1)} %compare_and_fusion), kind=kOutput, calls=%fused_computation.3 | convolution fusion | flops 101466112 | bytes 1999104 | tf_op jit(solution)/shard_map/dot_general | solution.py:50
  122.8 5.4 %all-to-all-done.2 = f32[16,1,512]{2,1,0:T(1,128)} async-done(((f32[16,1,512]{2,1,0:T(1,128)}), f32[16,1,512]{2,1,0:T(1,128)}, u32[]{:S(2)}, u32[]{:S(2)}) %all-to-all-start.2) | async-done | bytes 32800 | tf_op jit(solution)/shard_map/all_to_all | solution.py:21
  128.1 0.5 broadcast.27
  128.7 2.1 %reduce = f32[16,512]{1,0:T(8,128)} reduce(f32[16,1,512]{2,1,0:T(1,128)} %all-to-all-done.2, f32[]{:T(128)} %broadcast.27), dimensions={1}, to_apply=%all_to_all.21.reduce_sub_computation | reduce | bytes 65540 | tf_op jit(solution)/shard_map/all_to_all | solution.py:21
  130.7 1.4 %reshape.59 = f32[16,8,64]{2,1,0:T(8,128)} reshape(f32[16,512]{1,0:T(8,128)} %reduce) | data formatting | bytes 65536
  132.2 1.5 %bitcast_reduce_fusion = f32[64,8]{0,1:T(8,128)} fusion(f32[16,8,64]{2,1,0:T(8,128)} %reshape.59), kind=kLoop, calls=%fused_computation.28 | loop fusion | flops 7680 | bytes 34816 | tf_op jit(solution)/shard_map/reduce_sum | solution.py:22
  (1 shorter events, 0.0 us)
Async XLA Ops:
  0.6 17.4 %copy-start = (bf16[3,3,3,256,256]{4,3,2,1,0:T(8,128)(2,1)S(1)}, bf16[3,3,3,256,256]{4,3,2,1,0:T(8,128)(2,1)}, u32[]{:S(2)}) copy-start(bf16[3,3,3,256,256]{4,3,2,1,0:T(8,128)(2,1)} %param.7) | copy-start | bytes 10616836
  2.0 14.6 %collective-permute-start = (bf16[1,2,32,16,256]{4,2,3,1,0:T(8,128)(2,1)S(1)}, bf16[1,2,32,16,256]{4,2,3,1,0:T(8,128)(2,1)S(1)}, u32[]{:S(2)}, u32[]{:S(2)}) collective-permute-start(bf16[1,2,32,16,256]{4,2,3,1,0:T(8,128)(2,1)S(1)} %copy.27), channel_id=1, source_target_pairs={{0,2},{2,4},{4,6},{6,8},{8,10},{10,12},{12,14},{14,16},{16,18},{18... | collective-permute-start | bytes 1572872 | tf_op jit(solution)/shard_map/ppermute | solution.py:10
  17.8 0.7 copy-start.3
  24.7 1.0 copy-start.1
  25.7 0.7 copy-start.2
  34.1 19.1 %all-to-all-start = ((bf16[16,2,512]{2,1,0:T(2,128)(2,1)}), bf16[16,2,512]{2,1,0:T(2,128)(2,1)}, u32[]{:S(2)}, u32[]{:S(2)}) async-start(bf16[16,2,512]{2,1,0:T(2,128)(2,1)} %reshape.56), calls=%async_computation | async-start | bytes 65536 | tf_op jit(solution)/shard_map/all_to_all | solution.py:47
  115.9 12.3 %all-to-all-start.2 = ((f32[16,1,512]{2,1,0:T(1,128)}), f32[16,1,512]{2,1,0:T(1,128)}, u32[]{:S(2)}, u32[]{:S(2)}) async-start(f32[16,1,512]{2,1,0:T(1,128)} %reshape.58), calls=%async_computation.2 | async-start | bytes 65536 | tf_op jit(solution)/shard_map/all_to_all | solution.py:21
where the time goes:
time: 135 us; the launch traced here: 134 us
  blocking collectives  50.7 us (38%)
  waiting for transfers between devices  23.3 us (17%)
  local copies, waits for them, and re-layouts  21.6 us (16%)
  starting transfers between devices  18.4 us (14%)
  matrix products  11.8 us (9%)
  other arithmetic  7.04 us (5%)
    all_to_all x1, blocking collectives, summed_on_arrival(): pieces = lax.all_to_all(split_up(value, dim, peers), axis, 0, 0, tiled=True)  50.7 us
    all_to_all x1, starting transfers between devices, local(): lax.all_to_all(patches, 'seq', split_axis=1, concat_axis=0, tiled=True)  10.9 us
    unnamed x14, local copies, waits for them, and re-layouts  9.97 us
    ppermute x1, waiting for transfers between devices, passed_along(): lax.ppermute(value, axis, [(source, source + steps) for source in range(i...  9.76 us
    all_to_all x1, waiting for transfers between devices, local(): lax.all_to_all(patches, 'seq', split_axis=1, concat_axis=0, tiled=True)  8.18 us
    conv_general_dilated x1, matrix products, local(): lax.conv_general_dilated(widened, conv_weight, (1, 1, 1), ((0, 0), (1, 1)...  6.25 us
    all_to_all x1, waiting for transfers between devices, summed_on_arrival(): pieces = lax.all_to_all(split_up(value, dim, peers), axis, 0, 0, tiled=True)  5.35 us
    all_to_all x1, starting transfers between devices, summed_on_arrival(): pieces = lax.all_to_all(split_up(value, dim, peers), axis, 0, 0, tiled=True)  4.13 us
  transfers between devices with their start and end apart: 3, of which 3 were waited for; matrix products, arithmetic and copies ran while one was open for 3% of the time, Pallas kernels for 0%

commit v1 on v0

v1 whole, which is shorter than its diff:
```python
import jax
import jax.numpy as jnp
from jax import lax
from jax.experimental import pallas as pl
from jax.experimental.pallas import tpu as pltpu
from jax.sharding import PartitionSpec as P

MESH = pl.DeviceIdType.MESH
BF16, F32 = jnp.bfloat16, jnp.float32
NX, NY, NZH, NZL = 4, 8, 3, 4
NZ = NZH * NZL
N_SEQ, N_MP = 16, 2
GROUP = N_SEQ * N_MP
FRAMES = 32


def div(a, b):
    return lax.div(a, jnp.int32(b))


def rem(a, b):
    return lax.rem(a, jnp.int32(b))


def kernel(
    feat_hbm, w_hbm, wl_hbm, order_hbm, emb_hbm, cot_hbm,
    embedded_ref, grad_ref,
    feat, w, wl, order, emb, cot, halo, shifted, acc, act, wl4, perm_t, perm, cot_t,
    tokbuf, tokin, gsend, xrecv, ysend, yrecv, zsend, zrecv,
    load_sem, halo_send, halo_recv, tok_send, tok_recv,
    x_send, x_recv, y_send, y_recv, z_send, z_recv,
):
    dp, seq, mp = lax.axis_index("dp"), lax.axis_index("seq"), lax.axis_index("mp")
    x, zl = rem(seq, NX), div(seq, NX)
    y, zh = rem(dp, NY), div(dp, NY)
    z = zh * NZL + zl
    me = seq * N_MP + mp
    frame = me + 1
    slab_peer = seq + 2 * mp - 1
    has_peer = jnp.logical_and(slab_peer >= 0, slab_peer < N_SEQ)
    partner = (dp, seq, 1 - mp)

    def x_peer(k):
        tx = rem(x + k, NX)
        return tx, (dp, zl * NX + tx, mp)

    def y_peer(k):
        ty = rem(y + k, NY)
        return ty, (zh * NY + ty, seq, mp)

    def z_peer(k):
        tz = rem(z + k, NZ)
        th, tl = div(tz, NZL), rem(tz, NZL)
        return th * 2 + div(tl, 2), (th * NY + y, tl * NX + x, mp)

    def group_peer(k):
        index = rem(me + k, GROUP)
        return div(index, N_MP), (dp, div(index, N_MP), rem(index, N_MP))

    loads = [
        pltpu.make_async_copy(src, dst, load_sem.at[i])
        for i, (src, dst) in enumerate(
            [(feat_hbm.at[0], feat), (w_hbm, w), (wl_hbm, wl), (order_hbm, order), (cot_hbm, cot), (emb_hbm, emb)]
        )
    ]
    for load in loads:
        load.start()

    barrier = pltpu.get_barrier_semaphore()

    def greet(k, carry):
        pl.semaphore_signal(barrier, inc=1, device_id=group_peer(k)[1], device_id_type=MESH)
        return carry

    lax.fori_loop(1, GROUP, greet, 0)
    for k in range(1, NY):
        pl.semaphore_signal(barrier, inc=1, device_id=y_peer(k)[1], device_id_type=MESH)
    for k in range(1, NZ):
        pl.semaphore_signal(barrier, inc=1, device_id=z_peer(k)[1], device_id_type=MESH)
    loads[0].wait()
    pl.semaphore_wait(barrier, GROUP - 1 + NY - 1 + NZ - 1)

    halo_copy = pltpu.make_async_remote_copy(
        src_ref=feat.at[mp], dst_ref=halo, send_sem=halo_send, recv_sem=halo_recv,
        device_id=(dp, slab_peer, 1 - mp), device_id_type=MESH,
    )

    @pl.when(has_peer)
    def _():
        halo_copy.start()

    def shift(slot, value):
        value = value.astype(F32)
        zero = jnp.zeros((FRAMES, 1, 256), F32)
        shifted[slot, 0, 1:33] = jnp.concatenate([zero, value[:, :15]], axis=1).astype(BF16)
        shifted[slot, 1, 1:33] = value.astype(BF16)
        shifted[slot, 2, 1:33] = jnp.concatenate([value[:, 1:], zero], axis=1).astype(BF16)

    for slot in range(3):
        for dx in range(3):
            shifted[slot, dx, 0] = jnp.zeros((16, 256), BF16)
            shifted[slot, dx, 33] = jnp.zeros((16, 256), BF16)

    def taps(slot, dt):
        total = None
        for dy in range(3):
            for dx in range(3):
                part = jnp.dot(
                    shifted[slot, dx, dy : dy + 32].reshape(512, 256), w[dt, dy, dx],
                    preferred_element_type=F32,
                )
                total = part if total is None else total + part
        return total.reshape(32, 16, 256)

    shift(0, feat[0])
    shift(1, feat[1])
    loads[1].wait()
    acc[0] = taps(0, 1 - mp) + taps(1, 2 - mp)
    acc[1] = jnp.zeros((32, 16, 256), F32)

    loads[2].wait()
    wl4[...] = jnp.zeros((4, 64, 256), BF16)
    for k in range(4):
        wl4[k, 16 * k : 16 * k + 16] = wl[...]
    loads[3].wait()
    hot = jnp.where(lax.broadcasted_iota(jnp.int32, (256, 256), 0) == order[...], 1.0, 0.0).astype(F32)
    perm_t[...] = hot.astype(BF16)
    perm[...] = hot.T.astype(BF16)

    first = frame == 1

    @pl.when(has_peer)
    def _():
        halo_copy.wait_recv()

    @pl.when(jnp.logical_not(has_peer))
    def _():
        halo[...] = jnp.zeros((32, 16, 256), BF16)

    shift(2, halo[...])
    slot3 = jnp.where(first, 0, 2)
    dt3 = jnp.where(first, 2, 2 * mp)
    dst3 = jnp.where(first, 1, 0)
    acc[dst3] += taps(slot3, dt3)

    def to_tokens(slot, source):
        value = source.astype(F32) + jax.nn.silu(acc[slot])
        for c in range(2):
            act[c] = value[:, :, 128 * c : 128 * c + 128]
        total = None
        for dx in range(2):
            half = jnp.concatenate(
                [act[c, :, pl.ds(dx, 8, stride=2), :] for c in range(2)], axis=-1
            ).reshape(16, 2, 8, 256)
            for dy in range(2):
                part = lax.dot_general(
                    half[:, dy].reshape(128, 256).astype(BF16), wl4[2 * dy + dx],
                    (((1,), (1,)), ((), ())), preferred_element_type=F32,
                )
                total = part if total is None else total + part
        tokbuf[slot] = total.reshape(16, 8, 64).astype(BF16)

    def token_copy(slot, to, k):
        band, device = group_peer(k)
        return pltpu.make_async_remote_copy(
            src_ref=tokbuf.at[slot, band], dst_ref=tokin.at[to],
            send_sem=tok_send.at[slot, k], recv_sem=tok_recv.at[to],
            device_id=device, device_id_type=MESH,
        )

    def send_tokens(slot, to):
        def step(k, carry):
            token_copy(slot, to, k).start()
            return carry

        lax.fori_loop(1, GROUP, step, 0)
        tokin[to] = tokbuf[slot, seq]

    @pl.when(mp == 0)
    def _():
        to_tokens(0, feat[1])

    @pl.when(mp == 1)
    def _():
        to_tokens(0, halo[...])

    @pl.when(frame < FRAMES)
    def _():
        send_tokens(0, frame)

    @pl.when(first)
    def _():
        to_tokens(1, feat[0])
        send_tokens(1, 0)

    loads[4].wait()
    for block in range(NY * NZH):
        moved = jnp.dot(perm_t[...], cot[:, 128 * block : 128 * block + 128], preferred_element_type=F32)
        turned = moved.T.reshape(2, 2, NX, 8, 256)
        for one in range(2):
            for tx in range(NX):
                cot_t[one, tx, block % NY, block // NY] = jnp.concatenate(
                    [turned[0, one, tx], turned[1, one, tx]], axis=0
                ).astype(BF16)

    def token_wait(f, carry):
        own = jnp.logical_or(frame == f, jnp.logical_and(first, f == 0))

        @pl.when(jnp.logical_not(own))
        def _():
            pltpu.make_async_remote_copy(
                src_ref=tokbuf.at[0, 0], dst_ref=tokin.at[f],
                send_sem=tok_send.at[0, 0], recv_sem=tok_recv.at[f],
                device_id=partner, device_id_type=MESH,
            ).wait_recv()

        return carry

    lax.fori_loop(0, FRAMES, token_wait, 0)
    tok = tokin[...].astype(F32).reshape(256, 64)
    zero = jnp.zeros((256, 64), F32)
    tok_a = jnp.concatenate([tok, zero], axis=1).astype(BF16)
    tok_b = jnp.concatenate([zero, tok], axis=1).astype(BF16)

    def x_copy(k):
        tx, device = x_peer(k)
        return pltpu.make_async_remote_copy(
            src_ref=gsend.at[tx], dst_ref=xrecv.at[k - 1],
            send_sem=x_send.at[k - 1], recv_sem=x_recv.at[k - 1],
            device_id=device, device_id_type=MESH,
        )

    for k in (2, 1, 3, 0):
        tx = rem(x + k, NX)
        gsend[tx] = (
            jnp.dot(cot_t[0, tx].reshape(384, 256), tok_a, preferred_element_type=F32)
            + jnp.dot(cot_t[1, tx].reshape(384, 256), tok_b, preferred_element_type=F32)
        ).astype(BF16)
        if k:
            x_copy(k).start()

    loads[5].wait()
    ordered = jnp.dot(perm[...], tok.astype(BF16), preferred_element_type=F32).astype(BF16)
    for c in range(0, 3072, 512):
        embedded_ref[:, c : c + 512] = jnp.dot(
            ordered, emb[:, c : c + 512], preferred_element_type=F32
        ).astype(BF16)

    for k in range(1, NX):
        x_copy(k).wait_recv()
    total = gsend[x].astype(F32)
    for k in range(1, NX):
        total += xrecv[k - 1].astype(F32)
    ysend[...] = total.reshape(NY, 48, 128).astype(BF16)

    def y_copy(k):
        ty, device = y_peer(k)
        return pltpu.make_async_remote_copy(
            src_ref=ysend.at[ty], dst_ref=yrecv.at[k - 1],
            send_sem=y_send.at[k - 1], recv_sem=y_recv.at[k - 1],
            device_id=device, device_id_type=MESH,
        )

    for k in (4, 3, 5, 2, 6, 1, 7):
        y_copy(k).start()
    for k in range(1, NY):
        y_copy(k).wait_recv()
    total = ysend[y].astype(F32)
    for k in range(1, NY):
        total += yrecv[k - 1].astype(F32)
    zsend[...] = total.reshape(6, 8, 128).astype(BF16)

    def z_copy(k):
        piece, device = z_peer(k)
        return pltpu.make_async_remote_copy(
            src_ref=zsend.at[piece], dst_ref=zrecv.at[k - 1],
            send_sem=z_send.at[k - 1], recv_sem=z_recv.at[k - 1],
            device_id=device, device_id_type=MESH,
        )

    for k in (6, 5, 7, 4, 8, 3, 9, 2, 10, 1, 11):
        z_copy(k).start()
    for k in range(1, NZ):
        z_copy(k).wait_recv()
    total = zsend[zh * 2 + div(zl, 2)].astype(F32)
    for k in range(1, NZ):
        total += zrecv[k - 1].astype(F32)
    grad_ref[...] = jnp.where(rem(zl, 2) == 0, total[:, :64], total[:, 64:])

    @pl.when(has_peer)
    def _():
        halo_copy.wait_send()

    def drain(slot, to):
        def step(k, carry):
            token_copy(slot, to, k).wait_send()
            return carry

        lax.fori_loop(1, GROUP, step, 0)

    @pl.when(frame < FRAMES)
    def _():
        drain(0, frame)

    @pl.when(first)
    def _():
        drain(1, 0)

    for k in range(1, NX):
        x_copy(k).wait_send()
    for k in range(1, NY):
        y_copy(k).wait_send()
    for k in range(1, NZ):
        z_copy(k).wait_send()


def local(features, conv_weight, latent_weight, order, embed_weight, cotangent):
    dma = pltpu.SemaphoreType.DMA
    embedded, grad = pl.pallas_call(
        kernel,
        name="section",
        out_shape=(
            jax.ShapeDtypeStruct((256, 3072), BF16),
            jax.ShapeDtypeStruct((8, 64), F32),
        ),
        in_specs=[pl.BlockSpec(memory_space=pl.ANY)] * 6,
        out_specs=(pl.BlockSpec(memory_space=pltpu.VMEM),) * 2,
        scratch_shapes=[
            pltpu.VMEM((2, 32, 16, 256), BF16),
            pltpu.VMEM((3, 3, 3, 256, 256), BF16),
            pltpu.VMEM((16, 256), BF16),
            pltpu.VMEM((1, 256), jnp.int32),
            pltpu.VMEM((64, 3072), BF16),
            pltpu.VMEM((256, 3072), BF16),
            pltpu.VMEM((32, 16, 256), BF16),
            pltpu.VMEM((3, 3, 34, 16, 256), BF16),
            pltpu.VMEM((2, 32, 16, 256), F32),
            pltpu.VMEM((2, 32, 16, 128), F32),
            pltpu.VMEM((4, 64, 256), BF16),
            pltpu.VMEM((256, 256), BF16),
            pltpu.VMEM((256, 256), BF16),
            pltpu.VMEM((2, NX, NY, NZH, 16, 256), BF16),
            pltpu.VMEM((2, 16, 8, 64), BF16),
            pltpu.VMEM((32, 8, 64), BF16),
            pltpu.VMEM((NX, 384, 128), BF16),
            pltpu.VMEM((NX - 1, 384, 128), BF16),
            pltpu.VMEM((NY, 48, 128), BF16),
            pltpu.VMEM((NY - 1, 48, 128), BF16),
            pltpu.VMEM((6, 8, 128), BF16),
            pltpu.VMEM((NZ - 1, 8, 128), BF16),
            dma((6,)),
            dma, dma,
            dma((2, GROUP)), dma((FRAMES,)),
            dma((NX - 1,)), dma((NX - 1,)),
            dma((NY - 1,)), dma((NY - 1,)),
            dma((NZ - 1,)), dma((NZ - 1,)),
        ],
        compiler_params=pltpu.CompilerParams(collective_id=0, has_side_effects=True),
    )(features, conv_weight, latent_weight.T, order.reshape(1, 256), embed_weight, cotangent)
    return embedded, grad.T[None]


def solution(mesh):
    placed = (
        P("dp", "seq", None, None, None),
        P(),
        P(),
        P(),
        P(None, "mp"),
        P(("dp", "seq"), "mp"),
    )
    return jax.shard_map(
        local,
        mesh=mesh,
        in_specs=placed,
        out_specs=(P(("dp", "seq"), "mp"), P("mp", None, ("dp", "seq"))),
        check_vma=False,
    )
```

time: 135 us -> 56.6 us (0.42)
  Pallas kernels: 0 us -> 52.6 us
  blocking collectives: 50.7 us -> 0 us
  waiting for transfers between devices: 23.3 us -> 0 us
  starting transfers between devices: 18.4 us -> 0 us
  local copies, waits for them, and re-layouts: 21.6 us -> 3.25 us
  matrix products: 11.8 us -> 0 us
  other arithmetic: 7.04 us -> 0 us
    pallas_call x0 -> x1, Pallas kernels: none -> 52.6 us  [local(): pl.pallas_call(kernel, name='section', out_shape=(jax.ShapeDtypeStruct((2...]
    all_to_all x1 -> x0, blocking collectives: 50.7 us -> none  [summed_on_arrival(): pieces = lax.all_to_all(split_up(value, dim, peers), axis, 0, 0, tiled=True)]
    all_to_all x2 -> x0, starting transfers between devices: 15 us -> none  [the longest x1 10.9 us: local(): lax.all_to_all(patches, 'seq', split_axis=1, concat_axis=0, tiled=True)]
    all_to_all x2 -> x0, waiting for transfers between devices: 13.5 us -> none  [the longest x1 8.18 us: local(): lax.all_to_all(patches, 'seq', split_axis=1, concat_axis=0, tiled=True)]
    ppermute x1 -> x0, waiting for transfers between devices: 9.76 us -> none  [passed_along(): lax.ppermute(value, axis, [(source, source + steps) for source in range(i...]
    unnamed x14 -> x4, local copies, waits for them, and re-layouts: 9.97 us -> 3.25 us
    conv_general_dilated x1 -> x0, matrix products: 6.25 us -> none  [local(): lax.conv_general_dilated(widened, conv_weight, (1, 1, 1), ((0, 0), (1, 1)...]
    dot_general x3 -> x0, matrix products: 5.6 us -> none  [the longest x1 2.79 us: local(): jnp.dot(tokens, embed_weight, preferred_element_type=jnp.float32)]
  transfers between devices with their start and end apart: 3 -> 0, of which waited for: 3 -> 0; matrix products, arithmetic and copies ran while one was open for 3% -> 0% of each run, Pallas kernels for 0% -> 0%
where the time goes in v1:
time: 56.6 us; the launch traced here: 56.5 us
  Pallas kernels  52.6 us (93%)
  local copies, waits for them, and re-layouts  3.25 us (6%)
  between operations  0.65 us (1%)
    pallas_call x1, Pallas kernels, local(): pl.pallas_call(kernel, name='section', out_shape=(jax.ShapeDtypeStruct((2...  52.6 us
    unnamed x4, local copies, waits for them, and re-layouts  3.25 us

profile of v1, /device:TPU:8, one launch (start us, length us, event | category | flops | bytes accessed | tf_op | source)
XLA Modules:
  0.0 56.5 jit_solution(3906663377180076529)
XLA Ops:
  0.6 52.6 %section.1 = (bf16[256,3072]{1,0:T(8,128)(2,1)}, f32[8,64]{1,0:T(8,128)}) custom-call(bf16[1,2,32,16,256]{4,3,2,1,0:T(8,128)(2,1)} %feat_hbm.1, bf16[3,3,3,256,256]{4,3,2,1,0:T(8,128)(2,1)} %w_hbm.1, bf16[16,256]{1,0:T(8,128)(2,1)} %bitcast.5, s32[1,256]{1,0:T(1,128)} %bitcast.7, bf16[64,3072]{1,0:T(8,128)(2,1)} %emb_hbm.1, bf16[256,3072]{1,0:T(8,128)(2,1)} %cot_hbm.1), custom_call_target="tpu_custom_call" | custom-call | tf_op jit(solution)/shard_map/section/pallas_call | solution.py:319
  53.2 0.0 copy-start
  53.2 2.7 %copy.10 = bf16[256,3072]{1,0:T(8,128)(2,1)} copy(bf16[256,3072]{1,0:T(8,128)(2,1)} %get-tuple-element.8) | data formatting | bytes 3145728
  55.9 0.0 copy-done
  55.9 0.6 %copy.11 = f32[1,64,8]{1,2,0:T(8,128)} copy(f32[1,64,8]{1,2,0:T(8,128)S(1)} %bitcast.6) | data formatting | bytes 4096
Async XLA Ops:
  53.2 2.7 %copy-start = (f32[8,64]{1,0:T(8,128)S(1)}, f32[8,64]{1,0:T(8,128)}, u32[]{:S(2)}) copy-start(f32[8,64]{1,0:T(8,128)} %get-tuple-element.5) | copy-start | bytes 6148

commit v2 on v1

--- a/solution.py
+++ b/solution.py
@@ -23,9 +23,9 @@
 
 
 def kernel(
-    feat_hbm, w_hbm, wl_hbm, order_hbm, emb_hbm, cot_hbm,
+    feat_hbm, w_hbm, wl_hbm, order_hbm, cot_hbm, emb_hbm,
     embedded_ref, grad_ref,
-    feat, w, wl, order, emb, cot, halo, shifted, acc, act, wl4, perm_t, perm, cot_t,
+    feat, w, wl, order, cot, emb, halo, shifted, acc, act, wl4, perm_t, perm, cot_t,
     tokbuf, tokin, gsend, xrecv, ysend, yrecv, zsend, zrecv,
     load_sem, halo_send, halo_recv, tok_send, tok_recv,
     x_send, x_recv, y_send, y_recv, z_send, z_recv,
@@ -48,10 +48,8 @@
         ty = rem(y + k, NY)
         return ty, (zh * NY + ty, seq, mp)
 
-    def z_peer(k):
-        tz = rem(z + k, NZ)
-        th, tl = div(tz, NZL), rem(tz, NZL)
-        return th * 2 + div(tl, 2), (th * NY + y, tl * NX + x, mp)
+    def z_device(tz):
+        return div(tz, NZL) * NY + y, rem(tz, NZL) * NX + x, mp
 
     def group_peer(k):
         index = rem(me + k, GROUP)
@@ -76,7 +74,7 @@
     for k in range(1, NY):
         pl.semaphore_signal(barrier, inc=1, device_id=y_peer(k)[1], device_id_type=MESH)
     for k in range(1, NZ):
-        pl.semaphore_signal(barrier, inc=1, device_id=z_peer(k)[1], device_id_type=MESH)
+        pl.semaphore_signal(barrier, inc=1, device_id=z_device(rem(z + k, NZ)), device_id_type=MESH)
     loads[0].wait()
     pl.semaphore_wait(barrier, GROUP - 1 + NY - 1 + NZ - 1)
 
@@ -194,14 +192,16 @@
         send_tokens(1, 0)
 
     loads[4].wait()
-    for block in range(NY * NZH):
-        moved = jnp.dot(perm_t[...], cot[:, 128 * block : 128 * block + 128], preferred_element_type=F32)
-        turned = moved.T.reshape(2, 2, NX, 8, 256)
-        for one in range(2):
-            for tx in range(NX):
-                cot_t[one, tx, block % NY, block // NY] = jnp.concatenate(
-                    [turned[0, one, tx], turned[1, one, tx]], axis=0
-                ).astype(BF16)
+    for block in range(NZH * NY // 2):
+        zh_of, y_of = block // (NY // 2), 2 * (block % (NY // 2))
+        moved = jnp.dot(perm_t[...], cot[:, 256 * block : 256 * block + 256], preferred_element_type=F32)
+        turned = moved.T.reshape(2, 2, 2, NX, 8, 256)
+        for pair in range(2):
+            for one in range(2):
+                for tx in range(NX):
+                    cot_t[2 * zh_of + pair, one, tx, 8 * y_of : 8 * y_of + 16] = jnp.concatenate(
+                        [turned[0, pair, one, tx], turned[1, pair, one, tx]], axis=0
+                    ).astype(BF16)
 
     def token_wait(f, carry):
         own = jnp.logical_or(frame == f, jnp.logical_and(first, f == 0))
@@ -222,70 +222,74 @@
     tok_a = jnp.concatenate([tok, zero], axis=1).astype(BF16)
     tok_b = jnp.concatenate([zero, tok], axis=1).astype(BF16)
 
-    def x_copy(k):
+    far_first = (3, 2, 4, 1, 5, 0)
+    pair = div(z, 2)
+
+    def x_copy(o, k):
         tx, device = x_peer(k)
         return pltpu.make_async_remote_copy(
-            src_ref=gsend.at[tx], dst_ref=xrecv.at[k - 1],
-            send_sem=x_send.at[k - 1], recv_sem=x_recv.at[k - 1],
+            src_ref=gsend.at[o, tx], dst_ref=xrecv.at[o, k - 1],
+            send_sem=x_send.at[o, k - 1], recv_sem=x_recv.at[o, k - 1],
             device_id=device, device_id_type=MESH,
         )
 
-    for k in (2, 1, 3, 0):
-        tx = rem(x + k, NX)
-        gsend[tx] = (
-            jnp.dot(cot_t[0, tx].reshape(384, 256), tok_a, preferred_element_type=F32)
-            + jnp.dot(cot_t[1, tx].reshape(384, 256), tok_b, preferred_element_type=F32)
-        ).astype(BF16)
-        if k:
-            x_copy(k).start()
+    for o, off in enumerate(far_first):
+        c = rem(pair + off, NZ // 2)
+        gsend[o] = (
+            jnp.dot(cot_t[c, 0].reshape(256, 256), tok_a, preferred_element_type=F32)
+            + jnp.dot(cot_t[c, 1].reshape(256, 256), tok_b, preferred_element_type=F32)
+        ).astype(BF16).reshape(NX, 64, 128)
+        for k in (2, 1, 3):
+            x_copy(o, k).start()
 
     loads[5].wait()
     ordered = jnp.dot(perm[...], tok.astype(BF16), preferred_element_type=F32).astype(BF16)
-    for c in range(0, 3072, 512):
-        embedded_ref[:, c : c + 512] = jnp.dot(
-            ordered, emb[:, c : c + 512], preferred_element_type=F32
+    for i in range(0, 3072, 512):
+        embedded_ref[:, i : i + 512] = jnp.dot(
+            ordered, emb[:, i : i + 512], preferred_element_type=F32
         ).astype(BF16)
 
-    for k in range(1, NX):
-        x_copy(k).wait_recv()
-    total = gsend[x].astype(F32)
-    for k in range(1, NX):
-        total += xrecv[k - 1].astype(F32)
-    ysend[...] = total.reshape(NY, 48, 128).astype(BF16)
-
-    def y_copy(k):
+    def y_copy(o, k):
         ty, device = y_peer(k)
         return pltpu.make_async_remote_copy(
-            src_ref=ysend.at[ty], dst_ref=yrecv.at[k - 1],
-            send_sem=y_send.at[k - 1], recv_sem=y_recv.at[k - 1],
+            src_ref=ysend.at[o, ty], dst_ref=yrecv.at[o, k - 1],
+            send_sem=y_send.at[o, k - 1], recv_sem=y_recv.at[o, k - 1],
             device_id=device, device_id_type=MESH,
         )
 
-    for k in (4, 3, 5, 2, 6, 1, 7):
-        y_copy(k).start()
-    for k in range(1, NY):
-        y_copy(k).wait_recv()
-    total = ysend[y].astype(F32)
-    for k in range(1, NY):
-        total += yrecv[k - 1].astype(F32)
-    zsend[...] = total.reshape(6, 8, 128).astype(BF16)
-
-    def z_copy(k):
-        piece, device = z_peer(k)
+    for o in range(6):
+        total = gsend[o, x].astype(F32)
+        for k in range(1, NX):
+            x_copy(o, k).wait_recv()
+            total += xrecv[o, k - 1].astype(F32)
+        ysend[o] = total.reshape(NY, 8, 128).astype(BF16)
+        for k in (4, 3, 5, 2, 6, 1, 7):
+            y_copy(o, k).start()
+
+    def z_copy(o, tz, k):
         return pltpu.make_async_remote_copy(
-            src_ref=zsend.at[piece], dst_ref=zrecv.at[k - 1],
+            src_ref=zsend.at[o], dst_ref=zrecv.at[k - 1],
             send_sem=z_send.at[k - 1], recv_sem=z_recv.at[k - 1],
-            device_id=device, device_id_type=MESH,
-        )
-
-    for k in (6, 5, 7, 4, 8, 3, 9, 2, 10, 1, 11):
-        z_copy(k).start()
+            device_id=z_device(tz), device_id_type=MESH,
+        )
+
+    def z_targets(o):
+        c = rem(pair + far_first[o], NZ // 2)
+        both = [2 * c, 2 * c + 1] if far_first[o] else [z + 1 - 2 * rem(z, 2)]
+        return [(tz, rem(tz - z + NZ, NZ)) for tz in both]
+
+    for o in range(6):
+        total = ysend[o, y].astype(F32)
+        for k in range(1, NY):
+            y_copy(o, k).wait_recv()
+            total += yrecv[o, k - 1].astype(F32)
+        zsend[o] = total.astype(BF16)
+        for tz, k in z_targets(o):
+            z_copy(o, tz, k).start()
     for k in range(1, NZ):
-        z_copy(k).wait_recv()
-    total = zsend[zh * 2 + div(zl, 2)].astype(F32)
-    for k in range(1, NZ):
+        z_copy(0, rem(z + k, NZ), k).wait_recv()
         total += zrecv[k - 1].astype(F32)
-    grad_ref[...] = jnp.where(rem(zl, 2) == 0, total[:, :64], total[:, 64:])
+    grad_ref[...] = jnp.where(rem(z, 2) == 0, total[:, :64], total[:, 64:])
 
     @pl.when(has_peer)
     def _():
@@ -306,32 +310,45 @@
     def _():
         drain(1, 0)
 
-    for k in range(1, NX):
-        x_copy(k).wait_send()
-    for k in range(1, NY):
-        y_copy(k).wait_send()
+    for o in range(6):
+        for k in range(1, NX):
+            x_copy(o, k).wait_send()
+        for k in range(1, NY):
+            y_copy(o, k).wait_send()
     for k in range(1, NZ):
-        z_copy(k).wait_send()
+        z_copy(0, rem(z + k, NZ), k).wait_send()
+
+
+def finish(embedded_ref, partial_ref, embedded_hbm, grad_hbm, sem):
+    copies = [
+        pltpu.make_async_copy(embedded_ref, embedded_hbm, sem.at[0]),
+        pltpu.make_async_copy(partial_ref, grad_hbm, sem.at[1]),
+    ]
+    for copy in copies:
+        copy.start()
+    for copy in copies:
+        copy.wait()
 
 
 def local(features, conv_weight, latent_weight, order, embed_weight, cotangent):
     dma = pltpu.SemaphoreType.DMA
-    embedded, grad = pl.pallas_call(
+    vmem = pl.BlockSpec(memory_space=pltpu.VMEM)
+    embedded, partial = pl.pallas_call(
         kernel,
         name="section",
         out_shape=(
             jax.ShapeDtypeStruct((256, 3072), BF16),
             jax.ShapeDtypeStruct((8, 64), F32),
         ),
-        in_specs=[pl.BlockSpec(memory_space=pl.ANY)] * 6,
-        out_specs=(pl.BlockSpec(memory_space=pltpu.VMEM),) * 2,
+        in_specs=[pl.BlockSpec(memory_space=pltpu.HBM)] * 6,
+        out_specs=(vmem, vmem),
         scratch_shapes=[
             pltpu.VMEM((2, 32, 16, 256), BF16),
             pltpu.VMEM((3, 3, 3, 256, 256), BF16),
             pltpu.VMEM((16, 256), BF16),
             pltpu.VMEM((1, 256), jnp.int32),
+            pltpu.VMEM((256, 3072), BF16),
             pltpu.VMEM((64, 3072), BF16),
-            pltpu.VMEM((256, 3072), BF16),
             pltpu.VMEM((32, 16, 256), BF16),
             pltpu.VMEM((3, 3, 34, 16, 256), BF16),
             pltpu.VMEM((2, 32, 16, 256), F32),
@@ -339,24 +356,43 @@
             pltpu.VMEM((4, 64, 256), BF16),
             pltpu.VMEM((256, 256), BF16),
             pltpu.VMEM((256, 256), BF16),
-            pltpu.VMEM((2, NX, NY, NZH, 16, 256), BF16),
+            pltpu.VMEM((6, 2, NX, 64, 256), BF16),
             pltpu.VMEM((2, 16, 8, 64), BF16),
             pltpu.VMEM((32, 8, 64), BF16),
-            pltpu.VMEM((NX, 384, 128), BF16),
-            pltpu.VMEM((NX - 1, 384, 128), BF16),
-            pltpu.VMEM((NY, 48, 128), BF16),
-            pltpu.VMEM((NY - 1, 48, 128), BF16),
+            pltpu.VMEM((6, NX, 64, 128), BF16),
+            pltpu.VMEM((6, NX - 1, 64, 128), BF16),
+            pltpu.VMEM((6, NY, 8, 128), BF16),
+            pltpu.VMEM((6, NY - 1, 8, 128), BF16),
             pltpu.VMEM((6, 8, 128), BF16),
             pltpu.VMEM((NZ - 1, 8, 128), BF16),
             dma((6,)),
             dma, dma,
             dma((2, GROUP)), dma((FRAMES,)),
-            dma((NX - 1,)), dma((NX - 1,)),
-            dma((NY - 1,)), dma((NY - 1,)),
+            dma((6, NX - 1)), dma((6, NX - 1)),
+            dma((6, NY - 1)), dma((6, NY - 1)),
             dma((NZ - 1,)), dma((NZ - 1,)),
         ],
-        compiler_params=pltpu.CompilerParams(collective_id=0, has_side_effects=True),
-    )(features, conv_weight, latent_weight.T, order.reshape(1, 256), embed_weight, cotangent)
+        compiler_params=pltpu.CompilerParams(
+            collective_id=0, has_side_effects=True, vmem_limit_bytes=32 * 1024 * 1024
+        ),
+    )(
+        *(
+            pltpu.with_memory_space_constraint(value, pltpu.HBM)
+            for value in (features, conv_weight, latent_weight.T, order.reshape(1, 256), cotangent, embed_weight)
+        )
+    )
+    embedded, grad = pl.pallas_call(
+        finish,
+        name="finish",
+        out_shape=(
+            jax.ShapeDtypeStruct((256, 3072), BF16),
+            jax.ShapeDtypeStruct((8, 64), F32),
+        ),
+        in_specs=[vmem] * 2,
+        out_specs=(pl.BlockSpec(memory_space=pltpu.HBM),) * 2,
+        scratch_shapes=[dma((2,))],
+        compiler_params=pltpu.CompilerParams(vmem_limit_bytes=16 * 1024 * 1024),
+    )(embedded, partial)
     return embedded, grad.T[None]
 
 

time: 56.6 us -> 50.9 us (0.90)
  local copies, waits for them, and re-layouts: 3.25 us -> 0 us
  Pallas kernels: 52.6 us -> 50.1 us
    pallas_call x1, Pallas kernels: 52.6 us -> 49 us  [local(): pl.pallas_call(kernel, name='section', out_shape=(jax.ShapeDtypeStruct((2...]
    unnamed x4 -> x0, local copies, waits for them, and re-layouts: 3.25 us -> none
    pallas_call x0 -> x1, Pallas kernels: none -> 1.16 us  [local(): pl.pallas_call(finish, name='finish', out_shape=(jax.ShapeDtypeStruct((25...]
where the time goes in v2:
time: 50.9 us; the launch traced here: 50.8 us
  Pallas kernels  50.1 us (98%)
  between operations  0.64 us (1%)
    pallas_call x1, Pallas kernels, local(): pl.pallas_call(kernel, name='section', out_shape=(jax.ShapeDtypeStruct((2...  49 us
    pallas_call x1, Pallas kernels, local(): pl.pallas_call(finish, name='finish', out_shape=(jax.ShapeDtypeStruct((25...  1.16 us

profile of v2, /device:TPU:8, one launch (start us, length us, event | category | flops | bytes accessed | tf_op | source)
XLA Modules:
  0.0 50.8 jit_solution(9167904158329408435)
XLA Ops:
  0.6 49.0 %section.1 = (bf16[256,3072]{1,0:T(8,128)(2,1)S(1)}, f32[8,64]{1,0:T(8,128)S(1)}) custom-call(bf16[1,2,32,16,256]{4,3,2,1,0:T(8,128)(2,1)} %feat_hbm.1, bf16[3,3,3,256,256]{4,3,2,1,0:T(8,128)(2,1)} %w_hbm.1, bf16[16,256]{1,0:T(8,128)(2,1)} %bitcast.5, s32[1,256]{1,0:T(1,128)} %bitcast.6, bf16[256,3072]{1,0:T(8,128)(2,1)} %cot_hbm.1, bf16[64,3072]{1,0:T(8,128)(2,1)} %emb_hbm.1), custom_call_target="tpu_custom_call" | custom-call | tf_op jit(solution)/shard_map/section/pallas_call | solution.py:336
  49.6 1.2 %finish.1 = (bf16[256,3072]{1,0:T(8,128)(2,1)}, f32[8,64]{1,0:T(8,128)}) custom-call(bf16[256,3072]{1,0:T(8,128)(2,1)S(1)} %get-tuple-element.6.embedded_ref, f32[8,64]{1,0:T(8,128)S(1)} %get-tuple-element.7.partial_ref), custom_call_target="tpu_custom_call" | custom-call | tf_op jit(solution)/shard_map/finish/pallas_call | solution.py:384

commit v3 on v2

v3 whole, which is shorter than its diff:
```python
import jax
import jax.numpy as jnp
from jax import lax
from jax.experimental import pallas as pl
from jax.experimental.pallas import tpu as pltpu
from jax.sharding import PartitionSpec as P

MESH = pl.DeviceIdType.MESH
BF16, F32 = jnp.bfloat16, jnp.float32
NX, NY, NZH, NZL = 4, 8, 3, 4
NZ = NZH * NZL
N_SEQ, N_MP = 16, 2
GROUP = N_SEQ * N_MP
FRAMES = 32
DEPTH = 6


def div(a, b):
    return lax.div(a, jnp.int32(b))


def rem(a, b):
    return lax.rem(a, jnp.int32(b))


def kernel(
    feat_hbm, w_hbm, wl_hbm, order_hbm, cot_hbm, emb_hbm,
    embedded_ref, grad_ref,
    feat, w, wl, order, cot, emb, halo, shifted, acc, act, wl4, perm_t, perm, cot_t,
    tokbuf, tokin, gsend, xrecv, ysend, yzrecv,
    load_sem, halo_send, halo_recv, tok_send, tok_recv,
    x_send, x_recv, yz_send, yz_recv, met,
):
    dp, seq, mp = lax.axis_index("dp"), lax.axis_index("seq"), lax.axis_index("mp")
    x, zl = rem(seq, NX), div(seq, NX)
    y, zh = rem(dp, NY), div(dp, NY)
    z = zh * NZL + zl
    me = seq * N_MP + mp
    frame = me + 1
    slab_peer = seq + 2 * mp - 1
    has_peer = jnp.logical_and(slab_peer >= 0, slab_peer < N_SEQ)
    partner = (dp, seq, 1 - mp)

    def x_peer(k):
        tx = rem(x + k, NX)
        return tx, (dp, zl * NX + tx, mp)

    def member(index):
        return div(index, N_MP), (dp, div(index, N_MP), rem(index, N_MP))

    loads = [
        pltpu.make_async_copy(src, dst, load_sem.at[i])
        for i, (src, dst) in enumerate(
            [(feat_hbm.at[0], feat), (w_hbm, w), (wl_hbm, wl), (order_hbm, order), (cot_hbm, cot), (emb_hbm, emb)]
        )
    ]
    for load in loads:
        load.start()

    def line_device(dy, dz):
        ty, tz = rem(y + dy + NY, NY), rem(z + dz + NZ, NZ)
        return div(tz, NZL) * NY + ty, rem(tz, NZL) * NX + x, mp

    def signal(sem, device):
        pl.semaphore_signal(sem, inc=1, device_id=device, device_id_type=MESH)

    def tell(sem, offsets):
        for dy, dz in offsets:
            signal(sem, line_device(dy, dz))

    near = [(0, 1), (0, -1), (1, 0), (-1, 0)]
    barrier = pltpu.get_barrier_semaphore()
    slab_device = (dp, slab_peer, 1 - mp)

    @pl.when(has_peer)
    def _():
        signal(barrier, slab_device)

    for k in range(1, NX):
        signal(barrier, (dp, zl * NX + rem(x + k, NX), mp))
    for k in range(NX):
        signal(barrier, (dp, zl * NX + rem(x + k, NX), 1 - mp))
    tell(barrier, near)
    loads[0].wait()
    pl.semaphore_wait(barrier, jnp.where(has_peer, 12, 11))

    parts = (slice(0, 17), slice(17, 32))
    halo_copies = [
        pltpu.make_async_remote_copy(
            src_ref=feat.at[mp, rows], dst_ref=halo.at[rows], send_sem=halo_send.at[h], recv_sem=halo_recv.at[h],
            device_id=slab_device, device_id_type=MESH,
        )
        for h, rows in enumerate(parts)
    ]

    @pl.when(has_peer)
    def _():
        for copy in halo_copies:
            copy.start()

    tell(met.at[0], near)

    def shift(slot, source, rows):
        value = source[rows].astype(F32)
        zero = jnp.zeros((rows.stop - rows.start, 1, 256), F32)
        put = slice(1 + rows.start, 1 + rows.stop)
        shifted[slot, 0, put] = jnp.concatenate([zero, value[:, :15]], axis=1).astype(BF16)
        shifted[slot, 1, put] = value.astype(BF16)
        shifted[slot, 2, put] = jnp.concatenate([value[:, 1:], zero], axis=1).astype(BF16)

    for slot in range(3):
        for dx in range(3):
            shifted[slot, dx, 0] = jnp.zeros((16, 256), BF16)
            shifted[slot, dx, 33] = jnp.zeros((16, 256), BF16)

    def taps(slot, dt, first_row, rows):
        total = None
        for dy in range(3):
            for dx in range(3):
                part = jnp.dot(
                    shifted[slot, dx, first_row + dy : first_row + dy + rows].reshape(16 * rows, 256),
                    w[dt, dy, dx], preferred_element_type=F32,
                )
                total = part if total is None else total + part
        return total.reshape(rows, 16, 256)

    shift(0, feat.at[0], slice(0, 32))
    shift(1, feat.at[1], slice(0, 32))
    loads[1].wait()
    acc[0] = taps(0, 1 - mp, 0, 32) + taps(1, 2 - mp, 0, 32)
    acc[1] = jnp.zeros((32, 16, 256), F32)

    pl.semaphore_wait(met.at[0], 4)
    tell(met.at[1], [(0, 2), (0, -2), (2, 0), (-2, 0)])

    loads[2].wait()
    wl4[...] = jnp.zeros((4, 128, 256), BF16)
    for k in range(4):
        wl4[k, 16 * k : 16 * k + 16] = wl[...]
    loads[3].wait()
    hot = jnp.where(lax.broadcasted_iota(jnp.int32, (256, 256), 0) == order[...], 1.0, 0.0).astype(F32)
    perm_t[...] = hot.astype(BF16)
    perm[...] = hot.T.astype(BF16)

    first = frame == 1
    slot3 = jnp.where(first, 0, 2)
    dt3 = jnp.where(first, 2, 2 * mp)
    dst3 = jnp.where(first, 1, 0)

    def to_tokens(slot, source, h):
        half = slice(16 * h, 16 * h + 16)
        value = source[half].astype(F32) + jax.nn.silu(acc[slot, half])
        for c in range(2):
            act[c] = value[:, :, 128 * c : 128 * c + 128]
        total = None
        for dx in range(2):
            columns = jnp.concatenate(
                [act[c, :, pl.ds(dx, 8, stride=2), :] for c in range(2)], axis=-1
            ).reshape(8, 2, 8, 256)
            for dy in range(2):
                part = lax.dot_general(
                    columns[:, dy].reshape(64, 256).astype(BF16), wl4[2 * dy + dx],
                    (((1,), (1,)), ((), ())), preferred_element_type=F32,
                )
                total = part if total is None else total + part
        tokbuf[slot, 8 * h : 8 * h + 8] = total.reshape(8, 8, 128).astype(BF16)

    def token_copy(slot, to, index):
        band, device = member(index)
        return pltpu.make_async_remote_copy(
            src_ref=tokbuf.at[slot, band], dst_ref=tokin.at[to],
            send_sem=tok_send.at[slot, index], recv_sem=tok_recv.at[to],
            device_id=device, device_id_type=MESH,
        )

    def send_tokens(slot, to, h):
        def step(k, carry):
            index = 16 * h + rem(me + k, 16)

            @pl.when(index != me)
            def _():
                token_copy(slot, to, index).start()

            return carry

        lax.fori_loop(0, 16, step, 0)

    pl.semaphore_wait(met.at[1], 4)
    tell(met.at[2], [(0, 4), (0, -4)])
    for h in range(2):
        @pl.when(has_peer)
        def _():
            halo_copies[h].wait_recv()

        @pl.when(jnp.logical_not(has_peer))
        def _():
            halo[parts[h]] = jnp.zeros((parts[h].stop - parts[h].start, 16, 256), BF16)

        shift(2, halo, parts[h])
        acc[dst3, 16 * h : 16 * h + 16] += taps(slot3, dt3, 16 * h, 16)

        @pl.when(mp == 0)
        def _():
            to_tokens(0, feat.at[1], h)

        @pl.when(mp == 1)
        def _():
            to_tokens(0, halo, h)

        @pl.when(frame < FRAMES)
        def _():
            send_tokens(0, frame, h)

        @pl.when(first)
        def _():
            to_tokens(1, feat.at[0], h)
            send_tokens(1, 0, h)

    @pl.when(frame < FRAMES)
    def _():
        tokin[frame] = tokbuf[0, seq]

    @pl.when(first)
    def _():
        tokin[0] = tokbuf[1, seq]

    pl.semaphore_wait(met.at[2], 2)
    tell(met.at[3], [(k, 0) for k in range(1, NY)])

    loads[4].wait()
    for block in range(NZH * NY // 2):
        zh_of, y_of = block // (NY // 2), 2 * (block % (NY // 2))
        moved = jnp.dot(perm_t[...], cot[:, 256 * block : 256 * block + 256], preferred_element_type=F32)
        turned = moved.T.reshape(2, 2, 2, NX, 8, 256)
        for pair in range(2):
            for one in range(2):
                for tx in range(NX):
                    cot_t[2 * zh_of + pair, one, tx, 8 * y_of : 8 * y_of + 16] = jnp.concatenate(
                        [turned[0, pair, one, tx], turned[1, pair, one, tx]], axis=0
                    ).astype(BF16)

    def token_wait(f, carry):
        own = jnp.logical_or(frame == f, jnp.logical_and(first, f == 0))

        @pl.when(jnp.logical_not(own))
        def _():
            pltpu.make_async_remote_copy(
                src_ref=tokbuf.at[0, 0], dst_ref=tokin.at[f],
                send_sem=tok_send.at[0, 0], recv_sem=tok_recv.at[f],
                device_id=partner, device_id_type=MESH,
            ).wait_recv()

        return carry

    lax.fori_loop(0, FRAMES, token_wait, 0)
    tok = tokin[...].astype(F32).reshape(256, 128)
    tok_a = tok.astype(BF16)
    tok_b = jnp.concatenate([tok[:, 64:], tok[:, :64]], axis=1).astype(BF16)

    far_first = (3, 2, 4, 1, 5, 0)
    pair = div(z, 2)

    def x_copy(o, k):
        tx, device = x_peer(k)
        return pltpu.make_async_remote_copy(
            src_ref=gsend.at[o, tx], dst_ref=xrecv.at[o, k - 1],
            send_sem=x_send.at[o, k - 1], recv_sem=x_recv.at[o, k - 1],
            device_id=device, device_id_type=MESH,
        )

    def send_x(o):
        c = rem(pair + far_first[o], NZ // 2)
        gsend[o] = (
            jnp.dot(cot_t[c, 0].reshape(256, 256), tok_a, preferred_element_type=F32)
            + jnp.dot(cot_t[c, 1].reshape(256, 256), tok_b, preferred_element_type=F32)
        ).astype(BF16).reshape(NX, 64, 128)
        for k in (2, 1, 3):
            x_copy(o, k).start()

    for o in range(DEPTH):
        send_x(o)

    loads[5].wait()
    ordered = jnp.dot(perm[...], tok_a, preferred_element_type=F32).astype(BF16)[:, :64]
    for i in range(0, 3072, 512):
        embedded_ref[:, i : i + 512] = jnp.dot(
            ordered, emb[:, i : i + 512], preferred_element_type=F32
        ).astype(BF16)

    def plane_copy(o, one, ky):
        tz = 2 * rem(pair + far_first[o], NZ // 2) + one
        slot = rem(tz - z + NZ, NZ) * NY + ky
        ty = rem(y + ky, NY)
        return slot, pltpu.make_async_remote_copy(
            src_ref=ysend.at[o, ty], dst_ref=yzrecv.at[slot],
            send_sem=yz_send.at[o, one, ky], recv_sem=yz_recv.at[slot],
            device_id=(div(tz, NZL) * NY + ty, rem(tz, NZL) * NX + x, mp), device_id_type=MESH,
        )

    def each_plane_copy(o, act_on):
        for ky in (4, 3, 5, 2, 6, 1, 7, 0):
            for one in range(2):
                slot, copy = plane_copy(o, one, ky)
                if far_first[o] or ky:
                    act_on(copy)
                else:
                    @pl.when(slot != 0)
                    def _():
                        act_on(copy)

    pl.semaphore_wait(met.at[3], NY - 1)
    for o in range(6):
        total = gsend[o, x].astype(F32)
        for k in range(1, NX):
            x_copy(o, k).wait_recv()
            total += xrecv[o, k - 1].astype(F32)
        ysend[o] = total.reshape(NY, 8, 128).astype(BF16)
        each_plane_copy(o, lambda copy: copy.start())

    total = ysend[5, y].astype(F32)
    for kz in (0, 1, 11, 2, 10, 3, 9, 4, 8, 5, 7, 6):
        for ky in (0, 1, 7, 2, 6, 3, 5, 4):
            slot = kz * NY + ky
            if slot:
                pltpu.make_async_remote_copy(
                    src_ref=ysend.at[0, 0], dst_ref=yzrecv.at[slot],
                    send_sem=yz_send.at[0, 0, 0], recv_sem=yz_recv.at[slot],
                    device_id=partner, device_id_type=MESH,
                ).wait_recv()
                total += yzrecv[slot].astype(F32)
    grad_ref[...] = jnp.where(rem(z, 2) == 0, total[:, :64], total[:, 64:])

    @pl.when(has_peer)
    def _():
        for copy in halo_copies:
            copy.wait_send()

    def drain(slot, to):
        def step(index, carry):
            @pl.when(index != me)
            def _():
                token_copy(slot, to, index).wait_send()

            return carry

        lax.fori_loop(0, GROUP, step, 0)

    @pl.when(frame < FRAMES)
    def _():
        drain(0, frame)

    @pl.when(first)
    def _():
        drain(1, 0)

    for o in range(6):
        for k in range(1, NX):
            x_copy(o, k).wait_send()
        each_plane_copy(o, lambda copy: copy.wait_send())


def finish(embedded_ref, partial_ref, embedded_hbm, grad_hbm, sem):
    copies = [
        pltpu.make_async_copy(embedded_ref, embedded_hbm, sem.at[0]),
        pltpu.make_async_copy(partial_ref, grad_hbm, sem.at[1]),
    ]
    for copy in copies:
        copy.start()
    for copy in copies:
        copy.wait()


def local(features, conv_weight, latent_weight, order, embed_weight, cotangent):
    dma = pltpu.SemaphoreType.DMA
    vmem = pl.BlockSpec(memory_space=pltpu.VMEM)
    embedded, partial = pl.pallas_call(
        kernel,
        name="section",
        out_shape=(
            jax.ShapeDtypeStruct((256, 3072), BF16),
            jax.ShapeDtypeStruct((8, 64), F32),
        ),
        in_specs=[pl.BlockSpec(memory_space=pltpu.HBM)] * 6,
        out_specs=(vmem, vmem),
        scratch_shapes=[
            pltpu.VMEM((2, 32, 16, 256), BF16),
            pltpu.VMEM((3, 3, 3, 256, 256), BF16),
            pltpu.VMEM((16, 256), BF16),
            pltpu.VMEM((1, 256), jnp.int32),
            pltpu.VMEM((256, 3072), BF16),
            pltpu.VMEM((64, 3072), BF16),
            pltpu.VMEM((32, 16, 256), BF16),
            pltpu.VMEM((3, 3, 34, 16, 256), BF16),
            pltpu.VMEM((2, 32, 16, 256), F32),
            pltpu.VMEM((2, 16, 16, 128), F32),
            pltpu.VMEM((4, 128, 256), BF16),
            pltpu.VMEM((256, 256), BF16),
            pltpu.VMEM((256, 256), BF16),
            pltpu.VMEM((6, 2, NX, 64, 256), BF16),
            pltpu.VMEM((2, 16, 8, 128), BF16),
            pltpu.VMEM((32, 8, 128), BF16),
            pltpu.VMEM((6, NX, 64, 128), BF16),
            pltpu.VMEM((6, NX - 1, 64, 128), BF16),
            pltpu.VMEM((6, NY, 8, 128), BF16),
            pltpu.VMEM((NZ * NY, 8, 128), BF16),
            dma((6,)),
            dma((2,)), dma((2,)),
            dma((2, GROUP)), dma((FRAMES,)),
            dma((6, NX - 1)), dma((6, NX - 1)),
            dma((6, 2, NY)), dma((NZ * NY,)),
            pltpu.SemaphoreType.REGULAR((4,)),
        ],
        compiler_params=pltpu.CompilerParams(
            collective_id=0, has_side_effects=True, vmem_limit_bytes=32 * 1024 * 1024
        ),
    )(
        *(
            pltpu.with_memory_space_constraint(value, pltpu.HBM)
            for value in (features, conv_weight, latent_weight.T, order.reshape(1, 256), cotangent, embed_weight)
        )
    )
    embedded, grad = pl.pallas_call(
        finish,
        name="finish",
        out_shape=(
            jax.ShapeDtypeStruct((256, 3072), BF16),
            jax.ShapeDtypeStruct((8, 64), F32),
        ),
        in_specs=[vmem] * 2,
        out_specs=(pl.BlockSpec(memory_space=pltpu.HBM),) * 2,
        scratch_shapes=[dma((2,))],
        compiler_params=pltpu.CompilerParams(vmem_limit_bytes=16 * 1024 * 1024),
    )(embedded, partial)
    return embedded, grad.T[None]


def solution(mesh):
    placed = (
        P("dp", "seq", None, None, None),
        P(),
        P(),
        P(),
        P(None, "mp"),
        P(("dp", "seq"), "mp"),
    )
    return jax.shard_map(
        local,
        mesh=mesh,
        in_specs=placed,
        out_specs=(P(("dp", "seq"), "mp"), P("mp", None, ("dp", "seq"))),
        check_vma=False,
    )
```

time: 50.9 us -> 47.6 us (0.935)
  Pallas kernels: 50.1 us -> 46.8 us
    pallas_call x1, Pallas kernels: 49 us -> 45.6 us  [local(): pl.pallas_call(kernel, name='section', out_shape=(jax.ShapeDtypeStruct((2...]
where the time goes in v3:
time: 47.6 us; the launch traced here: 47.4 us
  Pallas kernels  46.8 us (98%)
  between operations  0.64 us (1%)
    pallas_call x1, Pallas kernels, local(): pl.pallas_call(kernel, name='section', out_shape=(jax.ShapeDtypeStruct((2...  45.6 us
    pallas_call x1, Pallas kernels, local(): pl.pallas_call(finish, name='finish', out_shape=(jax.ShapeDtypeStruct((25...  1.16 us

profile of v3, /device:TPU:8, one launch (start us, length us, event | category | flops | bytes accessed | tf_op | source)
XLA Modules:
  0.0 47.4 jit_solution(12823876622726020124)
XLA Ops:
  0.6 45.6 %section.1 = (bf16[256,3072]{1,0:T(8,128)(2,1)S(1)}, f32[8,64]{1,0:T(8,128)S(1)}) custom-call(bf16[1,2,32,16,256]{4,3,2,1,0:T(8,128)(2,1)} %feat_hbm.1, bf16[3,3,3,256,256]{4,3,2,1,0:T(8,128)(2,1)} %w_hbm.1, bf16[16,256]{1,0:T(8,128)(2,1)} %bitcast.5, s32[1,256]{1,0:T(1,128)} %bitcast.6, bf16[256,3072]{1,0:T(8,128)(2,1)} %cot_hbm.1, bf16[64,3072]{1,0:T(8,128)(2,1)} %emb_hbm.1), custom_call_target="tpu_custom_call" | custom-call | tf_op jit(solution)/shard_map/section/pallas_call | solution.py:376
  46.3 1.2 %finish.1 = (bf16[256,3072]{1,0:T(8,128)(2,1)}, f32[8,64]{1,0:T(8,128)}) custom-call(bf16[256,3072]{1,0:T(8,128)(2,1)S(1)} %get-tuple-element.6.embedded_ref, f32[8,64]{1,0:T(8,128)S(1)} %get-tuple-element.7.partial_ref), custom_call_target="tpu_custom_call" | custom-call | tf_op jit(solution)/shard_map/finish/pallas_call | solution.py:422

commit v4 on v3

--- a/solution.py
+++ b/solution.py
@@ -48,13 +48,18 @@
     def member(index):
         return div(index, N_MP), (dp, div(index, N_MP), rem(index, N_MP))
 
+    frame_loads = [
+        pltpu.make_async_copy(feat_hbm.at[0, i], feat.at[i], load_sem.at[6 + j])
+        for j, i in enumerate((mp, 1 - mp))
+    ]
     loads = [
         pltpu.make_async_copy(src, dst, load_sem.at[i])
         for i, (src, dst) in enumerate(
-            [(feat_hbm.at[0], feat), (w_hbm, w), (wl_hbm, wl), (order_hbm, order), (cot_hbm, cot), (emb_hbm, emb)]
+            [(w_hbm, w), (wl_hbm, wl), (order_hbm, order), (cot_hbm, cot), (emb_hbm, emb)], 1
         )
     ]
-    for load in loads:
+    loads.insert(0, frame_loads[0])
+    for load in frame_loads:
         load.start()
 
     def line_device(dy, dz):
@@ -81,10 +86,12 @@
     for k in range(NX):
         signal(barrier, (dp, zl * NX + rem(x + k, NX), 1 - mp))
     tell(barrier, near)
+    for load in loads[1:4]:
+        load.start()
     loads[0].wait()
     pl.semaphore_wait(barrier, jnp.where(has_peer, 12, 11))
 
-    parts = (slice(0, 17), slice(17, 32))
+    parts = (slice(0, 9), slice(9, 17), slice(17, 25), slice(25, 32))
     halo_copies = [
         pltpu.make_async_remote_copy(
             src_ref=feat.at[mp, rows], dst_ref=halo.at[rows], send_sem=halo_send.at[h], recv_sem=halo_recv.at[h],
@@ -97,6 +104,9 @@
     def _():
         for copy in halo_copies:
             copy.start()
+
+    loads[4].start()
+    loads[5].start()
 
     tell(met.at[0], near)
 
@@ -124,6 +134,7 @@
                 total = part if total is None else total + part
         return total.reshape(rows, 16, 256)
 
+    frame_loads[1].wait()
     shift(0, feat.at[0], slice(0, 32))
     shift(1, feat.at[1], slice(0, 32))
     loads[1].wait()
@@ -188,16 +199,17 @@
     pl.semaphore_wait(met.at[1], 4)
     tell(met.at[2], [(0, 4), (0, -4)])
     for h in range(2):
-        @pl.when(has_peer)
-        def _():
-            halo_copies[h].wait_recv()
-
-        @pl.when(jnp.logical_not(has_peer))
-        def _():
-            halo[parts[h]] = jnp.zeros((parts[h].stop - parts[h].start, 16, 256), BF16)
-
-        shift(2, halo, parts[h])
-        acc[dst3, 16 * h : 16 * h + 16] += taps(slot3, dt3, 16 * h, 16)
+        for q in (2 * h, 2 * h + 1):
+            @pl.when(has_peer)
+            def _():
+                halo_copies[q].wait_recv()
+
+            @pl.when(jnp.logical_not(has_peer))
+            def _():
+                halo[parts[q]] = jnp.zeros((parts[q].stop - parts[q].start, 16, 256), BF16)
+
+            shift(2, halo, parts[q])
+            acc[dst3, 8 * q : 8 * q + 8] += taps(slot3, dt3, 8 * q, 8)
 
         @pl.when(mp == 0)
         def _():
@@ -316,6 +328,34 @@
             total += xrecv[o, k - 1].astype(F32)
         ysend[o] = total.reshape(NY, 8, 128).astype(BF16)
         each_plane_copy(o, lambda copy: copy.start())
+
+    @pl.when(has_peer)
+    def _():
+        for copy in halo_copies:
+            copy.wait_send()
+
+    def drain(slot, to):
+        def step(index, carry):
+            @pl.when(index != me)
+            def _():
+                token_copy(slot, to, index).wait_send()
+
+            return carry
+
+        lax.fori_loop(0, GROUP, step, 0)
+
+    @pl.when(frame < FRAMES)
+    def _():
+        drain(0, frame)
+
+    @pl.when(first)
+    def _():
+        drain(1, 0)
+
+    for o in range(6):
+        for k in range(1, NX):
+            x_copy(o, k).wait_send()
+        each_plane_copy(o, lambda copy: copy.wait_send())
 
     total = ysend[5, y].astype(F32)
     for kz in (0, 1, 11, 2, 10, 3, 9, 4, 8, 5, 7, 6):
@@ -330,40 +370,12 @@
                 total += yzrecv[slot].astype(F32)
     grad_ref[...] = jnp.where(rem(z, 2) == 0, total[:, :64], total[:, 64:])
 
-    @pl.when(has_peer)
-    def _():
-        for copy in halo_copies:
-            copy.wait_send()
-
-    def drain(slot, to):
-        def step(index, carry):
-            @pl.when(index != me)
-            def _():
-                token_copy(slot, to, index).wait_send()
-
-            return carry
-
-        lax.fori_loop(0, GROUP, step, 0)
-
-    @pl.when(frame < FRAMES)
-    def _():
-        drain(0, frame)
-
-    @pl.when(first)
-    def _():
-        drain(1, 0)
-
-    for o in range(6):
-        for k in range(1, NX):
-            x_copy(o, k).wait_send()
-        each_plane_copy(o, lambda copy: copy.wait_send())
-
 
 def finish(embedded_ref, partial_ref, embedded_hbm, grad_hbm, sem):
-    copies = [
-        pltpu.make_async_copy(embedded_ref, embedded_hbm, sem.at[0]),
-        pltpu.make_async_copy(partial_ref, grad_hbm, sem.at[1]),
-    ]
+    copies = [pltpu.make_async_copy(partial_ref, grad_hbm, sem.at[8])]
+    for i in range(8):
+        rows = pl.ds(32 * i, 32)
+        copies.append(pltpu.make_async_copy(embedded_ref.at[rows], embedded_hbm.at[rows], sem.at[i]))
     for copy in copies:
         copy.start()
     for copy in copies:
@@ -403,8 +415,8 @@
             pltpu.VMEM((6, NX - 1, 64, 128), BF16),
             pltpu.VMEM((6, NY, 8, 128), BF16),
             pltpu.VMEM((NZ * NY, 8, 128), BF16),
-            dma((6,)),
-            dma((2,)), dma((2,)),
+            dma((8,)),
+            dma((4,)), dma((4,)),
             dma((2, GROUP)), dma((FRAMES,)),
             dma((6, NX - 1)), dma((6, NX - 1)),
             dma((6, 2, NY)), dma((NZ * NY,)),
@@ -428,7 +440,7 @@
         ),
         in_specs=[vmem] * 2,
         out_specs=(pl.BlockSpec(memory_space=pltpu.HBM),) * 2,
-        scratch_shapes=[dma((2,))],
+        scratch_shapes=[dma((9,))],
         compiler_params=pltpu.CompilerParams(vmem_limit_bytes=16 * 1024 * 1024),
     )(embedded, partial)
     return embedded, grad.T[None]

time: 47.6 us -> 47.5 us (level)
  the two profiles are of different devices: /device:TPU:8 before, /device:TPU:2 now
where the time goes in v4:
time: 47.5 us; the launch traced here: 47.4 us
  Pallas kernels  46.7 us (98%)
  between operations  0.64 us (1%)
    pallas_call x1, Pallas kernels, local(): pl.pallas_call(kernel, name='section', out_shape=(jax.ShapeDtypeStruct((2...  45.5 us
    pallas_call x1, Pallas kernels, local(): pl.pallas_call(finish, name='finish', out_shape=(jax.ShapeDtypeStruct((25...  1.21 us

profile of v4, /device:TPU:2, one launch (start us, length us, event | category | flops | bytes accessed | tf_op | source)
XLA Modules:
  0.0 47.4 jit_solution(11713487271161343834)
XLA Ops:
  0.6 45.5 %section.1 = (bf16[256,3072]{1,0:T(8,128)(2,1)S(1)}, f32[8,64]{1,0:T(8,128)S(1)}) custom-call(bf16[1,2,32,16,256]{4,3,2,1,0:T(8,128)(2,1)} %feat_hbm.1, bf16[3,3,3,256,256]{4,3,2,1,0:T(8,128)(2,1)} %w_hbm.1, bf16[16,256]{1,0:T(8,128)(2,1)} %bitcast.5, s32[1,256]{1,0:T(1,128)} %bitcast.6, bf16[256,3072]{1,0:T(8,128)(2,1)} %cot_hbm.1, bf16[64,3072]{1,0:T(8,128)(2,1)} %emb_hbm.1), custom_call_target="tpu_custom_call" | custom-call | tf_op jit(solution)/shard_map/section/pallas_call | solution.py:388
  46.2 1.2 %finish.1 = (bf16[256,3072]{1,0:T(8,128)(2,1)}, f32[8,64]{1,0:T(8,128)}) custom-call(bf16[256,3072]{1,0:T(8,128)(2,1)S(1)} %get-tuple-element.6.embedded_ref, f32[8,64]{1,0:T(8,128)S(1)} %get-tuple-element.7.partial_ref), custom_call_target="tpu_custom_call" | custom-call | tf_op jit(solution)/shard_map/finish/pallas_call | solution.py:434
